TPU v7x, 128 devices: a whole 4x4x4 slice. The times are simulated.
128 devices in a mesh: row: 16 (over z, y_hi, core), col: 8 (over y_lo, x).
Axes of the slice: x: 4, y: 4 (y_hi: 2, y_lo: 2; y = y_hi * 2 + y_lo), z: 4, core: 2. Of those that a mesh axis runs over, the one named last changes fastest.
Arguments:
- left_prop: float32 [16, 8, 2, 512, 512], P('row', None, None, 'col'), may hold values from -0.1875 to 0.1875
- vertex: float32 [8, 2, 512, 512], P(None, None, ('row', 'col')), may hold values from -5 to 5
- right_prop: float32 [8, 16, 2, 512, 512], P(None, 'col', None, None, 'row'), may hold values from -0.1875 to 0.1875
- insertions: int32 [3], replicated, may hold values from 0 to 7
- window_start: int32 [2], replicated, may hold values from 0 to 255
Outputs:
- correlator: float32 [16, 16, 2, 512, 512], P('row', 'col')
Inputs may be any that keep to these rules, and one draw needn't show every extreme that they name: `insertions`: repeats may occur.
All inputs are finite; a program needn't handle non-finite values.
Results may differ from a plain program's by a relative error of at most 0.0001.
Values sent between devices are 32-bit elements; how exact they have to be, the bound alone decides.
No kernel may reach another device: no remote copies, remote signals or barrier semaphores. Data moves between devices by JAX's collectives and lax.ppermute only.
A program may use at most 128 MiB of HBM per device.

v0:
```python
import jax
import jax.numpy as jnp
from jax import lax
from jax.sharding import Mesh
from jax.sharding import PartitionSpec as P

NS = 8
LT = 256
ROW = ("row_0", "row_1", "row_2")
COL = ("col_0", "col_1")
ROW_COL = ("row_0", "row_1", "row_2", "col_0", "col_1")


def piece_ends(length, count):
    unit = 8 if length >= 8 * count else 1
    return [length // unit * k // count * unit for k in range(1, count)]


def all_blocks(x, axes, order):
    tiles = x[None]
    for k in order:
        tiles = lax.all_gather(tiles, axes[k], axis=0, tiled=True)
    held = [lax.axis_size(axes[k]) for k in reversed(order)]
    tiles = tiles.reshape(*held, *x.shape)
    turned = sorted(range(len(order)), key=lambda place: order[len(order) - 1 - place])
    return tiles.transpose(*turned, *range(len(order), tiles.ndim)).reshape(-1, *x.shape)


def in_order(tiles, dim):
    shape = list(tiles.shape[1:])
    shape[dim] *= tiles.shape[0]
    return jnp.moveaxis(tiles, 0, dim).reshape(shape)


def spread_gather(x, axes, dim):
    cut = max(range(max(1, x.ndim - 1)), key=lambda d: x.shape[d])
    count, finished = (len(axes), [])
    for leading, share in enumerate(jnp.split(x, piece_ends(x.shape[cut], count), axis=cut)):
        if share.size:
            order = [(leading - k) % count for k in range(count)]
            finished.append(all_blocks(share, axes, order))
    return in_order(jnp.concatenate(finished, axis=cut + 1), dim)


def complex_product(first, second):
    highest = lax.Precision.HIGHEST
    first_re, first_im = (first[..., 0, :, :], first[..., 1, :, :])
    second_re, second_im = (second[..., 0, :, :], second[..., 1, :, :])
    real_part = jnp.matmul(first_re, second_re, precision=highest) - jnp.matmul(
        first_im, second_im, precision=highest
    )
    imag_part = jnp.matmul(first_re, second_im, precision=highest) + jnp.matmul(
        first_im, second_re, precision=highest
    )
    return jnp.stack([real_part, imag_part], axis=-3)


def contract_with(left_operand, column_piece):
    summed = complex_product(left_operand[:, 0, None], column_piece[0][None])
    for which in range(1, column_piece.shape[0]):
        summed = summed + complex_product(left_operand[:, which, None], column_piece[which][None])
    return summed


def per_device(left_prop, vertex, right_prop, insertions, window_start):
    source_count = left_prop.shape[0]
    sink_count = right_prop.shape[1]
    source_slots = lax.axis_index(ROW) * source_count + jnp.arange(source_count, dtype=jnp.int32)
    sink_slots = lax.axis_index(COL) * sink_count + jnp.arange(sink_count, dtype=jnp.int32)
    slice_times = insertions * (LT // NS)
    source_times = (window_start[0] + source_slots) % LT
    sink_times = (window_start[1] + sink_slots) % LT
    left_sign = jnp.where(slice_times[None, :] < source_times[:, None], -1.0, 1.0).astype(
        jnp.float32
    )
    right_sign = jnp.where(sink_times[None, :] < slice_times[:, None], -1.0, 1.0).astype(
        jnp.float32
    )
    chosen_left = jnp.take(left_prop, insertions, axis=1) * left_sign[:, :, None, None, None]
    chosen_right = jnp.take(right_prop, insertions, axis=0) * right_sign[:, :, None, None, None]
    vertex_part = jnp.take(vertex, insertions, axis=0)
    vertex_full = spread_gather(vertex_part, ROW_COL, 2)
    left_full = lax.all_gather(chosen_left, COL, axis=3, tiled=True)
    vertex_right = complex_product(vertex_full[:, None], chosen_right)
    result = contract_with(left_full, lax.all_gather(vertex_right, ROW, axis=4, tiled=True))
    return result


def solution(mesh):
    finer = Mesh(mesh.devices.reshape(4, 2, 2, 2, 4), ("row_0", "row_1", "row_2", "col_0", "col_1"))
    return jax.shard_map(
        per_device,
        mesh=finer,
        in_specs=(
            P(ROW, None, None, COL, None),
            P(None, None, ROW_COL, None),
            P(None, COL, None, None, ROW),
            P(),
            P(),
        ),
        out_specs=P(ROW, COL, None, None, None),
        check_vma=False,
    )
```

profile of v0, /device:TPU:1, one launch (start us, length us, event | category | flops | bytes accessed | tf_op | source)
XLA Modules:
  0.0 401.7 jit_solution(11193293117327762396)
XLA Ops:
  8.0 1.5 gather_fusion.1
  9.6 5.5 %all-gather = f32[6,2,1,512]{3,1,2,0:T(2,128)S(1)} all-gather(f32[3,2,1,512]{3,1,2,0:T(2,128)S(1)} %copy.62), channel_id=2, replica_groups=mesh['row_0'=4,'row_1'=2,'row_2'=2,'col_0'=2,'col_1'=4] {'row_1'}, dimensions={0}, use_global_device_ids=true | all-gather | bytes 36864 | tf_op jit(solution)/shard_map/all_gather | solution.py:22
  15.1 10.3 %all_gather.68 = f32[8,3,2,1,512]{4,2,3,1,0:T(2,128)S(1)} all-gather(f32[2,3,2,1,512]{4,2,3,1,0:T(2,128)S(1)} %bitcast.186), channel_id=1, replica_groups=mesh['row_0'=4,'row_1'=2,'row_2'=2,'col_0'=2,'col_1'=4] {'row_0'}, dimensions={0}, use_global_device_ids=true | all-gather | bytes 122880 | tf_op jit(solution)/shard_map/all_gather | solution.py:22
  25.4 10.4 %all_gather.69 = f32[32,3,2,1,512]{4,2,3,1,0:T(2,128)S(1)} all-gather(f32[8,3,2,1,512]{4,2,3,1,0:T(2,128)S(1)} %all_gather.68), channel_id=1, replica_groups=mesh['row_0'=4,'row_1'=2,'row_2'=2,'col_0'=2,'col_1'=4] {'col_1'}, dimensions={0}, use_global_device_ids=true | all-gather | bytes 491520 | tf_op jit(solution)/shard_map/all_gather | solution.py:22
  35.9 7.4 %all_gather.70 = f32[64,3,2,1,512]{4,2,3,1,0:T(2,128)} all-gather(f32[32,3,2,1,512]{4,2,3,1,0:T(2,128)S(1)} %all_gather.69), channel_id=1, replica_groups=mesh['row_0'=4,'row_1'=2,'row_2'=2,'col_0'=2,'col_1'=4] {'col_0'}, dimensions={0}, use_global_device_ids=true | all-gather | bytes 1179648 | tf_op jit(solution)/shard_map/all_gather | solution.py:22
  43.4 9.9 %all-gather.1 = f32[6,2,1,512]{3,1,2,0:T(2,128)S(1)} all-gather(f32[3,2,1,512]{3,1,2,0:T(2,128)S(1)} %copy.65), channel_id=3, replica_groups=mesh['row_0'=4,'row_1'=2,'row_2'=2,'col_0'=2,'col_1'=4] {'row_2'}, dimensions={0}, use_global_device_ids=true | all-gather | bytes 36864 | tf_op jit(solution)/shard_map/all_gather | solution.py:22
  53.3 4.8 %all_gather.73 = f32[4,3,2,1,512]{4,2,3,1,0:T(2,128)S(1)} all-gather(f32[2,3,2,1,512]{4,2,3,1,0:T(2,128)S(1)} %bitcast.184), channel_id=1, replica_groups=mesh['row_0'=4,'row_1'=2,'row_2'=2,'col_0'=2,'col_1'=4] {'row_1'}, dimensions={0}, use_global_device_ids=true | all-gather | bytes 73728 | tf_op jit(solution)/shard_map/all_gather | solution.py:22
  58.1 9.2 %all_gather.74 = f32[16,3,2,1,512]{4,2,3,1,0:T(2,128)S(1)} all-gather(f32[4,3,2,1,512]{4,2,3,1,0:T(2,128)S(1)} %all_gather.73), channel_id=1, replica_groups=mesh['row_0'=4,'row_1'=2,'row_2'=2,'col_0'=2,'col_1'=4] {'row_0'}, dimensions={0}, use_global_device_ids=true | all-gather | bytes 245760 | tf_op jit(solution)/shard_map/all_gather | solution.py:22
  67.4 11.5 %all_gather.75 = f32[64,3,2,1,512]{4,2,3,1,0:T(2,128)} all-gather(f32[16,3,2,1,512]{4,2,3,1,0:T(2,128)S(1)} %all_gather.74), channel_id=1, replica_groups=mesh['row_0'=4,'row_1'=2,'row_2'=2,'col_0'=2,'col_1'=4] {'col_1'}, dimensions={0}, use_global_device_ids=true | all-gather | bytes 983040 | tf_op jit(solution)/shard_map/all_gather | solution.py:22
  78.9 3.6 all-gather.2
  82.5 9.5 %all_gather.78 = f32[4,3,2,1,512]{4,2,3,1,0:T(2,128)S(1)} all-gather(f32[2,3,2,1,512]{4,2,3,1,0:T(2,128)S(1)} %bitcast.185), channel_id=1, replica_groups=mesh['row_0'=4,'row_1'=2,'row_2'=2,'col_0'=2,'col_1'=4] {'row_2'}, dimensions={0}, use_global_device_ids=true | all-gather | bytes 73728 | tf_op jit(solution)/shard_map/all_gather | solution.py:22
  92.1 5.1 %all_gather.79 = f32[8,3,2,1,512]{4,2,3,1,0:T(2,128)S(1)} all-gather(f32[4,3,2,1,512]{4,2,3,1,0:T(2,128)S(1)} %all_gather.78), channel_id=1, replica_groups=mesh['row_0'=4,'row_1'=2,'row_2'=2,'col_0'=2,'col_1'=4] {'row_1'}, dimensions={0}, use_global_device_ids=true | all-gather | bytes 147456 | tf_op jit(solution)/shard_map/all_gather | solution.py:22
  97.2 10.7 %all_gather.80 = f32[32,3,2,1,512]{4,2,3,1,0:T(2,128)} all-gather(f32[8,3,2,1,512]{4,2,3,1,0:T(2,128)S(1)} %all_gather.79), channel_id=1, replica_groups=mesh['row_0'=4,'row_1'=2,'row_2'=2,'col_0'=2,'col_1'=4] {'row_0'}, dimensions={0}, use_global_device_ids=true | all-gather | bytes 491520 | tf_op jit(solution)/shard_map/all_gather | solution.py:22
  108.0 9.1 %all-gather.3 = f32[12,2,1,512]{3,1,2,0:T(2,128)S(1)} all-gather(f32[3,2,1,512]{3,1,2,0:T(2,128)S(1)} %copy.71), channel_id=5, replica_groups=mesh['row_0'=4,'row_1'=2,'row_2'=2,'col_0'=2,'col_1'=4] {'col_1'}, dimensions={0}, use_global_device_ids=true | all-gather | bytes 61440 | tf_op jit(solution)/shard_map/all_gather | solution.py:22
  117.2 3.9 all_gather.83
  121.1 9.2 %all_gather.84 = f32[16,3,2,1,512]{4,3,0,1,2:T(1,128)S(1)} all-gather(f32[8,3,2,1,512]{4,3,0,1,2:T(1,128)S(1)} %all_gather.83), channel_id=1, replica_groups=mesh['row_0'=4,'row_1'=2,'row_2'=2,'col_0'=2,'col_1'=4] {'row_2'}, dimensions={0}, use_global_device_ids=true | all-gather | bytes 294912 | tf_op jit(solution)/shard_map/all_gather | solution.py:22
  130.3 9.6 %all_gather.85 = f32[32,3,2,1,512]{4,3,0,1,2:T(1,128)} all-gather(f32[16,3,2,1,512]{4,3,0,1,2:T(1,128)S(1)} %all_gather.84), channel_id=1, replica_groups=mesh['row_0'=4,'row_1'=2,'row_2'=2,'col_0'=2,'col_1'=4] {'row_1'}, dimensions={0}, use_global_device_ids=true | all-gather | bytes 589824 | tf_op jit(solution)/shard_map/all_gather | solution.py:22
  141.9 1.1 fusion.17
  143.0 2.2 gather_fusion.2
  146.1 3.6 copy.64
  149.7 3.7 reshape.208
  153.4 3.6 copy.67
  157.0 4.3 %reshape.210 = f32[128,3,2,1,512]{4,3,0,1,2:T(1,128)} reshape(f32[4,2,2,2,4,3,2,1,512]{8,4,3,2,1,0,5,6,7:T(4,128)} %copy.67) | data formatting | bytes 3145728 | tf_op jit(solution)/shard_map/reshape | solution.py:26
  161.3 3.6 copy.70
  164.9 4.2 %reshape.212 = f32[128,3,2,1,512]{4,3,0,1,2:T(1,128)} reshape(f32[4,2,2,2,4,3,2,1,512]{8,4,3,2,1,0,5,6,7:T(4,128)} %copy.70) | data formatting | bytes 3145728 | tf_op jit(solution)/shard_map/reshape | solution.py:26
  169.1 3.9 all-gather.19.cloned.1.call-done
  173.0 8.6 %maximum_bitcast_fusion = f32[3,2,128,4,512]{4,3,2,0,1:T(4,128)} fusion(f32[128,3,2,1,512]{4,3,0,1,2:T(1,128)} %all-gather.19.cloned.1.call-done, f32[128,3,2,1,512]{4,3,0,1,2:T(1,128)} %reshape.212, f32[128,3,2,1,512]{4,3,0,1,2:T(1,128)} %reshape.210, f32[128,3,2,1,512]{4,3,0,1,2:T(1,128)S(1)} %reshape.208), kind=kLoop, calls=%fused_computation.3 | loop fusion | flops 4718592 | bytes 12582912 | tf_op jit(solution)/shard_map/transpose | solution.py:32
  181.6 8.2 %broadcast_in_dim_reshape.3 = f32[3,1,2,512,512]{4,3,0,2,1:T(8,128)} reshape(f32[3,2,128,4,512]{4,3,2,0,1:T(4,128)} %maximum_bitcast_fusion) | data formatting | bytes 12582912 | tf_op jit(solution)/shard_map/broadcast_in_dim;reshape | solution.py:84
  189.8 5.2 %fusion.1 = f32[3,512,64]{1,2,0:S(1)} fusion(f32[3,512,64]{1,2,0:T(8,128)S(1)} %bitcast.174, f32[3,1,2,512,512]{4,3,0,2,1:T(8,128)} %broadcast_in_dim_reshape.3), kind=kOutput, calls=%fused_computation.8 | convolution fusion | flops 603979776 | bytes 3932160
  195.1 5.1 %fusion.4 = f32[3,512,64]{1,2,0:S(1)} fusion(f32[3,512,64]{1,2,0:T(8,128)S(1)} %bitcast.175, f32[3,1,2,512,512]{4,3,0,2,1:T(8,128)} %broadcast_in_dim_reshape.3), kind=kOutput, calls=%fused_computation.11 | convolution fusion | flops 603979776 | bytes 3932160
  200.1 3.2 fusion.3
  203.3 3.2 fusion.2
  207.6 38.9 %all-gather.11.cloned.1.call-done = f32[1,3,2,512,512]{4,3,2,1,0:T(8,128)} async-done(((f32[1,3,2,64,512]{4,3,2,1,0:T(8,128)}), f32[1,3,2,512,512]{4,3,2,1,0:T(8,128)}) %all-gather.11.cloned.1.call-update) | async-done | bytes 6291472 | tf_op jit(solution)/shard_map/all_gather | solution.py:83
  246.5 92.3 %all-gather.21.cloned.1.call-done = f32[3,2,2,512,512]{3,4,1,0,2:T(8,128)} async-done(((f32[3,2,2,512,32]{3,4,1,0,2:T(8,128)}), f32[3,2,2,512,512]{3,4,1,0,2:T(8,128)}) %all-gather.21.cloned.1.call-update) | async-done | bytes 12582928 | tf_op jit(solution)/shard_map/all_gather | solution.py:85
  338.9 5.8 %fusion.13 = f32[512,2,512]{2,0,1:T(8,128)S(1)} fusion(f32[3,2,2,512,512]{3,4,1,0,2:T(8,128)} %all-gather.21.cloned.1.call-done, f32[1,3,2,512,512]{4,3,2,1,0:T(8,128)} %all-gather.11.cloned.1.call-done), kind=kOutput, calls=%fused_computation.32 | convolution fusion | flops 3221225472 | bytes 5242880 | tf_op jit(solution)/shard_map/dot_general | solution.py:52
  344.7 5.5 %fusion.9 = f32[512,2,512]{2,0,1:T(8,128)S(1)} fusion(f32[3,2,2,512,512]{3,4,1,0,2:T(8,128)} %all-gather.21.cloned.1.call-done, f32[1,3,2,512,512]{4,3,2,1,0:T(8,128)} %all-gather.11.cloned.1.call-done), kind=kOutput, calls=%fused_computation.28 | convolution fusion | flops 3221225472 | bytes 5242880 | tf_op jit(solution)/shard_map/dot_general | solution.py:52
  350.2 5.6 %fusion.5 = f32[512,2,512]{2,0,1:T(8,128)S(1)} fusion(f32[3,2,2,512,512]{3,4,1,0,2:T(8,128)} %all-gather.21.cloned.1.call-done, f32[1,3,2,512,512]{4,3,2,1,0:T(8,128)} %all-gather.11.cloned.1.call-done), kind=kOutput, calls=%fused_computation.24 | convolution fusion | flops 3221225472 | bytes 5242880 | tf_op jit(solution)/shard_map/dot_general | solution.py:52
  355.9 5.1 %fusion.14 = f32[512,2,512]{2,0,1:T(8,128)S(1)} fusion(f32[3,2,2,512,512]{3,4,1,0,2:T(8,128)S(1)} %copy-done.3, f32[1,3,2,512,512]{4,3,2,1,0:T(8,128)} %all-gather.11.cloned.1.call-done), kind=kOutput, calls=%fused_computation.33 | convolution fusion | flops 3221225472 | bytes 5242880 | tf_op jit(solution)/shard_map/dot_general | solution.py:49
  361.0 3.6 fusion.10
  364.6 3.6 fusion.6
  368.1 3.6 add_bitcast_fusion
  371.7 4.0 %add_bitcast_fusion.1 = f32[1,2,1,512,512]{4,3,1,2,0:T(8,128)S(1)} fusion(f32[512,2,512]{2,0,1:T(8,128)S(1)} %fusion.9, f32[3,2,2,512,512]{3,4,1,0,2:T(8,128)S(1)} %copy-done.3, f32[1,3,2,512,512]{4,3,2,1,0:T(8,128)S(1)} %copy-done.4), kind=kOutput, calls=%fused_computation.20 | convolution fusion | flops 3221749760 | bytes 7340032 | tf_op jit(solution)/shard_map/dot_general | solution.py:52
  375.8 3.6 add_bitcast_fusion.2
  379.4 3.6 subtract_bitcast_fusion
  383.0 3.8 subtract_bitcast_fusion.1
  386.8 3.7 subtract_bitcast_fusion.2
  390.6 1.6 fusion
  392.2 2.5 copy.86
  (48 shorter events, 5.1 us)
Async XLA Ops:
  6.5 134.7 %copy-start = (f32[1,8,2,64,512]{4,3,2,1,0:T(8,128)S(1)}, f32[1,8,2,64,512]{4,3,2,1,0:T(8,128)}, u32[]{:S(2)}) copy-start(f32[1,8,2,64,512]{4,3,2,1,0:T(8,128)} %param.5) | copy-start | bytes 6291460
  6.5 139.6 %all-gather.13.cloned.1.call-start = ((), (), s32[]{:S(2)}) async-start(), calls=%async_computation.1 | async-start | bytes 2359296 | tf_op jit(solution)/shard_map/all_gather | solution.py:22
  43.3 96.7 %copy-start.5 = (s32[2]{0:T(128)S(1)}, s32[2]{0:T(128)}, u32[]{:S(2)}) copy-start(s32[2]{0:T(128)} %param.9) | copy-start | bytes 28
  43.3 110.1 %all-gather.15.cloned.1.call-start = ((), (), s32[]{:S(2)}) async-start(), calls=%async_computation.2 | async-start | bytes 2359296 | tf_op jit(solution)/shard_map/all_gather | solution.py:22
  67.4 74.5 %copy-start.6 = (s32[3]{0:T(128)S(1)}, s32[3]{0:T(128)}, u32[]{:S(2)}) copy-start(s32[3]{0:T(128)} %param.8) | copy-start | bytes 40
  78.8 82.4 %all-gather.17.cloned.1.call-start = ((), (), s32[]{:S(2)}) async-start(), calls=%async_computation.3 | async-start | bytes 1966080 | tf_op jit(solution)/shard_map/all_gather | solution.py:22
  107.9 65.1 %all-gather.19.cloned.1.call-start = ((), (), s32[]{:S(2)}) async-start(), calls=%async_computation.4 | async-start | bytes 1966080 | tf_op jit(solution)/shard_map/all_gather | solution.py:22
  139.9 106.6 %all-gather.11.cloned.1.call-start = ((), (), s32[]{:S(2)}) async-start(), calls=%async_computation | async-start | bytes 7077888 | tf_op jit(solution)/shard_map/all_gather | solution.py:83
  142.9 195.9 %all-gather.21.cloned.1.call-start = ((), (), s32[]{:S(2)}) async-start(), calls=%async_computation.5 | async-start | bytes 13369344 | tf_op jit(solution)/shard_map/all_gather | solution.py:85
  189.8 10.3 %copy-start.2 = (f32[3,1,2,512,512]{4,3,0,2,1:T(8,128)S(1)}, f32[3,1,2,512,512]{4,3,0,2,1:T(8,128)}, u32[]{:S(2)}) copy-start(f32[3,1,2,512,512]{4,3,0,2,1:T(8,128)} %broadcast_in_dim_reshape.3) | copy-start | bytes 18874372
  338.9 17.0 %copy-start.3 = (f32[3,2,2,512,512]{3,4,1,0,2:T(8,128)S(1)}, f32[3,2,2,512,512]{3,4,1,0,2:T(8,128)}, u32[]{:S(2)}) copy-start(f32[3,2,2,512,512]{3,4,1,0,2:T(8,128)} %all-gather.21.cloned.1.call-done) | copy-start | bytes 37748740
  350.2 10.7 %copy-start.4 = (f32[1,3,2,512,512]{4,3,2,1,0:T(8,128)S(1)}, f32[1,3,2,512,512]{4,3,2,1,0:T(8,128)}, u32[]{:S(2)}) copy-start(f32[1,3,2,512,512]{4,3,2,1,0:T(8,128)} %all-gather.11.cloned.1.call-done) | copy-start | bytes 18874372
  390.6 4.1 %copy-start.1 = (f32[1,8,2,64,512]{4,3,2,1,0:T(8,128)S(1)}, f32[1,8,2,64,512]{4,3,2,1,0:T(8,128)}, u32[]{:S(2)}) copy-start(f32[1,8,2,64,512]{4,3,2,1,0:T(8,128)} %param.5) | copy-start | bytes 6291460
Sparse Core Ops, SparseCore 0:
  43.4 21.2 all-gather.12
  79.0 36.6 all-gather.14
  117.4 27.3 all-gather.16
  146.3 26.6 all-gather.18
  174.5 71.9 all-gather.10
  248.8 89.9 all-gather.20
where the time goes:
time: 406 us; the launch traced here: 402 us
  waiting for transfers between devices  135 us (33%)
  blocking collectives  130 us (32%)
  matrix products  68.2 us (17%)
  local copies, waits for them, and re-layouts  38.6 us (10%)
  other arithmetic  14.7 us (4%)
  between operations  14.7 us (4%)
    all_gather x16, blocking collectives, all_blocks(): tiles = lax.all_gather(tiles, axes[k], axis=0, tiled=True)  130 us
    all_gather x1, waiting for transfers between devices, per_device(): lax.all_gather(vertex_right, ROW, axis=4, tiled=True)  92.3 us
    all_gather x1, waiting for transfers between devices, per_device(): left_full = lax.all_gather(chosen_left, COL, axis=3, tiled=True)  38.9 us
    dot_general x3, matrix products, complex_product(): jnp.matmul(first_im, second_re, precision=highest)  17 us
    unnamed x4, matrix products  16.6 us
    reshape x3, local copies, waits for them, and re-layouts, all_blocks(): tiles.transpose(*turned, *range(len(order), tiles.ndim))  12.2 us
    dot_general x3, matrix products, complex_product(): jnp.matmul(first_re, second_re, precision=highest)  12.2 us
    dot_general x3, matrix products, complex_product(): jnp.matmul(first_re, second_im, precision=highest)  11.3 us
  transfers between devices with their start and end apart: 6, of which 3 were waited for; matrix products, arithmetic and copies ran while one was open for 16% of the time, Pallas kernels for 0%

commit v1 on v0

--- a/solution.py
+++ b/solution.py
@@ -9,6 +9,10 @@
 ROW = ("row_0", "row_1", "row_2")
 COL = ("col_0", "col_1")
 ROW_COL = ("row_0", "row_1", "row_2", "col_0", "col_1")
+
+
+def tokens_bring(mine_x, named_axis):
+    return jnp.concatenate(lax.all_gather(mine_x, named_axis), axis=4)
 
 
 def piece_ends(length, count):
@@ -82,7 +86,7 @@
     vertex_full = spread_gather(vertex_part, ROW_COL, 2)
     left_full = lax.all_gather(chosen_left, COL, axis=3, tiled=True)
     vertex_right = complex_product(vertex_full[:, None], chosen_right)
-    result = contract_with(left_full, lax.all_gather(vertex_right, ROW, axis=4, tiled=True))
+    result = contract_with(left_full, tokens_bring(vertex_right, ROW))
     return result
 
 

time: 406 us -> 433 us (1.067)
  local copies, waits for them, and re-layouts: 38.6 us -> 62 us
  waiting for transfers between devices: 135 us -> 142 us
    all_gather x0 -> x1, local copies, waits for them, and re-layouts: none -> 12 us  [tokens_bring(): return jnp.concatenate(lax.all_gather(mine_x, named_axis), axis=4)]
    slice x0 -> x1, local copies, waits for them, and re-layouts: none -> 10.6 us  [contract_with(): column_piece[which][None]]
    all_gather x1, waiting for transfers between devices: 38.9 us -> 48.1 us  [per_device(): left_full = lax.all_gather(chosen_left, COL, axis=3, tiled=True)]
    dot_general x3, matrix products: 17 us -> 12.3 us  [complex_product(): jnp.matmul(first_im, second_re, precision=highest)]
  transfers between devices with their start and end apart: 6 -> 6, of which waited for: 3 -> 3; matrix products, arithmetic and copies ran while one was open for 16% -> 12% of each run, Pallas kernels for 0% -> 0%
where the time goes in v1:
time: 433 us; the launch traced here: 429 us
  waiting for transfers between devices  142 us (33%)
  blocking collectives  130 us (30%)
  matrix products  65.4 us (15%)
  local copies, waits for them, and re-layouts  62 us (14%)
  other arithmetic  15.1 us (3%)
  between operations  14.7 us (3%)
    all_gather x16, blocking collectives, all_blocks(): tiles = lax.all_gather(tiles, axes[k], axis=0, tiled=True)  130 us
    all_gather x1, waiting for transfers between devices, tokens_bring(): return jnp.concatenate(lax.all_gather(mine_x, named_axis), axis=4)  88.6 us
    all_gather x1, waiting for transfers between devices, per_device(): left_full = lax.all_gather(chosen_left, COL, axis=3, tiled=True)  48.1 us
    unnamed x4, matrix products  16.6 us
    dot_general x3, matrix products, complex_product(): jnp.matmul(first_re, second_re, precision=highest)  14.5 us
    reshape x3, local copies, waits for them, and re-layouts, all_blocks(): tiles.transpose(*turned, *range(len(order), tiles.ndim))  13.3 us
    dot_general x3, matrix products, complex_product(): jnp.matmul(first_im, second_re, precision=highest)  12.3 us
    all_gather x1, local copies, waits for them, and re-layouts, tokens_bring(): return jnp.concatenate(lax.all_gather(mine_x, named_axis), axis=4)  12 us
  transfers between devices with their start and end apart: 6, of which 3 were waited for; matrix products, arithmetic and copies ran while one was open for 12% of the time, Pallas kernels for 0%

profile of v1, /device:TPU:1, one launch (start us, length us, event | category | flops | bytes accessed | tf_op | source)
XLA Modules:
  0.0 429.4 jit_solution(12857592787774247642)
XLA Ops:
  9.6 5.5 %all-gather = f32[6,2,1,512]{3,1,2,0:T(2,128)S(1)} all-gather(f32[3,2,1,512]{3,1,2,0:T(2,128)S(1)} %copy.43), channel_id=2, replica_groups=mesh['row_0'=4,'row_1'=2,'row_2'=2,'col_0'=2,'col_1'=4] {'row_1'}, dimensions={0}, use_global_device_ids=true | all-gather | bytes 36864 | tf_op jit(solution)/shard_map/all_gather | solution.py:26
  15.1 10.3 %all_gather.71 = f32[8,3,2,1,512]{4,2,3,1,0:T(2,128)S(1)} all-gather(f32[2,3,2,1,512]{4,2,3,1,0:T(2,128)S(1)} %bitcast.219), channel_id=1, replica_groups=mesh['row_0'=4,'row_1'=2,'row_2'=2,'col_0'=2,'col_1'=4] {'row_0'}, dimensions={0}, use_global_device_ids=true | all-gather | bytes 122880 | tf_op jit(solution)/shard_map/all_gather | solution.py:26
  25.4 10.4 %all_gather.72 = f32[32,3,2,1,512]{4,2,3,1,0:T(2,128)S(1)} all-gather(f32[8,3,2,1,512]{4,2,3,1,0:T(2,128)S(1)} %all_gather.71), channel_id=1, replica_groups=mesh['row_0'=4,'row_1'=2,'row_2'=2,'col_0'=2,'col_1'=4] {'col_1'}, dimensions={0}, use_global_device_ids=true | all-gather | bytes 491520 | tf_op jit(solution)/shard_map/all_gather | solution.py:26
  35.9 7.4 %all_gather.73 = f32[64,3,2,1,512]{4,2,3,1,0:T(2,128)} all-gather(f32[32,3,2,1,512]{4,2,3,1,0:T(2,128)S(1)} %all_gather.72), channel_id=1, replica_groups=mesh['row_0'=4,'row_1'=2,'row_2'=2,'col_0'=2,'col_1'=4] {'col_0'}, dimensions={0}, use_global_device_ids=true | all-gather | bytes 1179648 | tf_op jit(solution)/shard_map/all_gather | solution.py:26
  43.4 9.9 %all-gather.1 = f32[6,2,1,512]{3,1,2,0:T(2,128)S(1)} all-gather(f32[3,2,1,512]{3,1,2,0:T(2,128)S(1)} %copy.46), channel_id=3, replica_groups=mesh['row_0'=4,'row_1'=2,'row_2'=2,'col_0'=2,'col_1'=4] {'row_2'}, dimensions={0}, use_global_device_ids=true | all-gather | bytes 36864 | tf_op jit(solution)/shard_map/all_gather | solution.py:26
  53.3 4.8 %all_gather.76 = f32[4,3,2,1,512]{4,2,3,1,0:T(2,128)S(1)} all-gather(f32[2,3,2,1,512]{4,2,3,1,0:T(2,128)S(1)} %bitcast.217), channel_id=1, replica_groups=mesh['row_0'=4,'row_1'=2,'row_2'=2,'col_0'=2,'col_1'=4] {'row_1'}, dimensions={0}, use_global_device_ids=true | all-gather | bytes 73728 | tf_op jit(solution)/shard_map/all_gather | solution.py:26
  58.1 9.2 %all_gather.77 = f32[16,3,2,1,512]{4,2,3,1,0:T(2,128)S(1)} all-gather(f32[4,3,2,1,512]{4,2,3,1,0:T(2,128)S(1)} %all_gather.76), channel_id=1, replica_groups=mesh['row_0'=4,'row_1'=2,'row_2'=2,'col_0'=2,'col_1'=4] {'row_0'}, dimensions={0}, use_global_device_ids=true | all-gather | bytes 245760 | tf_op jit(solution)/shard_map/all_gather | solution.py:26
  67.4 11.3 %all_gather.78 = f32[64,3,2,1,512]{4,2,3,1,0:T(2,128)} all-gather(f32[16,3,2,1,512]{4,2,3,1,0:T(2,128)S(1)} %all_gather.77), channel_id=1, replica_groups=mesh['row_0'=4,'row_1'=2,'row_2'=2,'col_0'=2,'col_1'=4] {'col_1'}, dimensions={0}, use_global_device_ids=true | all-gather | bytes 983040 | tf_op jit(solution)/shard_map/all_gather | solution.py:26
  78.8 3.6 all-gather.2
  82.4 9.5 %all_gather.81 = f32[4,3,2,1,512]{4,2,3,1,0:T(2,128)S(1)} all-gather(f32[2,3,2,1,512]{4,2,3,1,0:T(2,128)S(1)} %bitcast.218), channel_id=1, replica_groups=mesh['row_0'=4,'row_1'=2,'row_2'=2,'col_0'=2,'col_1'=4] {'row_2'}, dimensions={0}, use_global_device_ids=true | all-gather | bytes 73728 | tf_op jit(solution)/shard_map/all_gather | solution.py:26
  91.9 5.1 %all_gather.82 = f32[8,3,2,1,512]{4,2,3,1,0:T(2,128)S(1)} all-gather(f32[4,3,2,1,512]{4,2,3,1,0:T(2,128)S(1)} %all_gather.81), channel_id=1, replica_groups=mesh['row_0'=4,'row_1'=2,'row_2'=2,'col_0'=2,'col_1'=4] {'row_1'}, dimensions={0}, use_global_device_ids=true | all-gather | bytes 147456 | tf_op jit(solution)/shard_map/all_gather | solution.py:26
  97.0 10.7 %all_gather.83 = f32[32,3,2,1,512]{4,2,3,1,0:T(2,128)} all-gather(f32[8,3,2,1,512]{4,2,3,1,0:T(2,128)S(1)} %all_gather.82), channel_id=1, replica_groups=mesh['row_0'=4,'row_1'=2,'row_2'=2,'col_0'=2,'col_1'=4] {'row_0'}, dimensions={0}, use_global_device_ids=true | all-gather | bytes 491520 | tf_op jit(solution)/shard_map/all_gather | solution.py:26
  107.9 9.1 %all-gather.3 = f32[12,2,1,512]{3,1,2,0:T(2,128)S(1)} all-gather(f32[3,2,1,512]{3,1,2,0:T(2,128)S(1)} %copy.52), channel_id=5, replica_groups=mesh['row_0'=4,'row_1'=2,'row_2'=2,'col_0'=2,'col_1'=4] {'col_1'}, dimensions={0}, use_global_device_ids=true | all-gather | bytes 61440 | tf_op jit(solution)/shard_map/all_gather | solution.py:26
  117.0 3.9 all_gather.86
  120.9 9.2 %all_gather.87 = f32[16,3,2,1,512]{4,3,0,1,2:T(1,128)S(1)} all-gather(f32[8,3,2,1,512]{4,3,0,1,2:T(1,128)S(1)} %all_gather.86), channel_id=1, replica_groups=mesh['row_0'=4,'row_1'=2,'row_2'=2,'col_0'=2,'col_1'=4] {'row_2'}, dimensions={0}, use_global_device_ids=true | all-gather | bytes 294912 | tf_op jit(solution)/shard_map/all_gather | solution.py:26
  130.2 9.6 %all_gather.88 = f32[32,3,2,1,512]{4,3,0,1,2:T(1,128)} all-gather(f32[16,3,2,1,512]{4,3,0,1,2:T(1,128)S(1)} %all_gather.87), channel_id=1, replica_groups=mesh['row_0'=4,'row_1'=2,'row_2'=2,'col_0'=2,'col_1'=4] {'row_1'}, dimensions={0}, use_global_device_ids=true | all-gather | bytes 589824 | tf_op jit(solution)/shard_map/all_gather | solution.py:26
  139.9 2.2 gather_fusion.2
  143.7 3.6 copy.45
  147.3 4.7 %reshape.215 = f32[128,3,2,1,512]{4,3,0,1,2:T(1,128)} reshape(f32[4,2,2,2,4,3,2,1,512]{8,4,3,2,1,0,5,6,7:T(4,128)} %copy.45) | data formatting | bytes 3145728 | tf_op jit(solution)/shard_map/reshape | solution.py:30
  152.0 3.6 copy.48
  155.5 4.3 %reshape.217 = f32[128,3,2,1,512]{4,3,0,1,2:T(1,128)} reshape(f32[4,2,2,2,4,3,2,1,512]{8,4,3,2,1,0,5,6,7:T(4,128)} %copy.48) | data formatting | bytes 3145728 | tf_op jit(solution)/shard_map/reshape | solution.py:30
  159.8 3.6 copy.51
  163.4 4.3 reshape.219
  167.7 5.2 %all-gather.20.cloned.1.call-done = f32[128,3,2,1,512]{4,3,0,1,2:T(1,128)} async-done(((f32[32,3,2,1,512]{4,3,0,1,2:T(1,128)}), f32[128,3,2,1,512]{4,3,0,1,2:T(1,128)}) %all-gather.20.cloned.1.call-update) | async-done | bytes 1572880 | tf_op jit(solution)/shard_map/all_gather | solution.py:26
  172.9 8.9 %maximum_bitcast_fusion = f32[3,2,128,4,512]{4,3,2,0,1:T(4,128)} fusion(f32[128,3,2,1,512]{4,3,0,1,2:T(1,128)} %all-gather.20.cloned.1.call-done, f32[128,3,2,1,512]{4,3,0,1,2:T(1,128)} %reshape.219, f32[128,3,2,1,512]{4,3,0,1,2:T(1,128)} %reshape.217, f32[128,3,2,1,512]{4,3,0,1,2:T(1,128)} %reshape.215), kind=kLoop, calls=%fused_computation.4 | loop fusion | flops 4718592 | bytes 12582912 | tf_op jit(solution)/shard_map/transpose | solution.py:36
  181.8 7.8 %broadcast_in_dim_reshape.3 = f32[3,1,2,512,512]{4,3,0,2,1:T(8,128)} reshape(f32[3,2,128,4,512]{4,3,2,0,1:T(4,128)} %maximum_bitcast_fusion) | data formatting | bytes 12582912 | tf_op jit(solution)/shard_map/broadcast_in_dim;reshape | solution.py:88
  189.7 5.2 %fusion.2 = f32[3,512,64]{1,2,0:S(1)} fusion(f32[3,512,64]{1,2,0:T(8,128)S(1)} %bitcast.207, f32[3,1,2,512,512]{4,3,0,2,1:T(8,128)} %broadcast_in_dim_reshape.3), kind=kOutput, calls=%fused_computation.10 | convolution fusion | flops 603979776 | bytes 3932160
  194.9 5.0 %fusion.3 = f32[3,512,64]{1,2,0:S(1)} fusion(f32[3,512,64]{1,2,0:T(8,128)S(1)} %bitcast.208, f32[3,1,2,512,512]{4,3,0,2,1:T(8,128)} %broadcast_in_dim_reshape.3), kind=kOutput, calls=%fused_computation.11 | convolution fusion | flops 603979776 | bytes 3932160
  199.9 3.2 fusion.4
  203.1 3.2 fusion.1
  210.0 88.6 %all-gather.22.cloned.1.call-done = f32[48,2,2,512,32]{3,4,1,0,2:T(8,128)} async-done(((f32[3,2,2,512,32]{3,4,1,0,2:T(8,128)}), f32[48,2,2,512,32]{3,4,1,0,2:T(8,128)}) %all-gather.22.cloned.1.call-update) | async-done | bytes 12582928 | tf_op jit(solution)/shard_map/all_gather | solution.py:15
  298.5 12.0 %copy.73 = f32[16,3,2,2,512,32]{4,5,0,3,2,1:T(8,128)} copy(f32[16,3,2,2,512,32]{4,5,2,1,0,3:T(8,128)} %bitcast.204) | data formatting | bytes 25165824 | tf_op jit(solution)/shard_map/all_gather | solution.py:15
  310.6 10.6 %fusion.20 = (f32[1,2,2,512,16,32]{3,5,4,2,1,0:T(8,128)}, f32[1,2,2,512,16,32]{3,5,4,2,1,0:T(8,128)}, f32[1,2,2,512,16,32]{3,5,4,2,1,0:T(8,128)}) fusion(f32[3,2,2,512,16,32]{3,5,4,2,1,0:T(8,128)} %bitcast.191), kind=kLoop, calls=%fused_computation.61 | loop fusion | bytes 25165824 | tf_op jit(solution)/shard_map/slice | solution.py:65
  321.1 48.1 %all-gather.12.cloned.1.call-done = f32[1,3,2,512,512]{4,3,2,1,0:T(8,128)} async-done(((f32[1,3,2,64,512]{4,3,2,1,0:T(8,128)}), f32[1,3,2,512,512]{4,3,2,1,0:T(8,128)}) %all-gather.12.cloned.1.call-update) | async-done | bytes 6291472 | tf_op jit(solution)/shard_map/all_gather | solution.py:87
  369.2 5.6 %fusion.14 = f32[512,2,512]{2,0,1:T(8,128)S(1)} fusion(f32[1,2,2,512,512]{3,4,2,1,0:T(8,128)} %bitcast.200, f32[1,3,2,512,512]{4,3,2,1,0:T(8,128)} %all-gather.12.cloned.1.call-done), kind=kOutput, calls=%fused_computation.34 | convolution fusion | flops 3221225472 | bytes 5242880 | tf_op jit(solution)/shard_map/dot_general | solution.py:53
  374.9 5.0 %fusion.13 = f32[512,2,512]{2,0,1:T(8,128)S(1)} fusion(f32[1,2,2,512,512]{3,4,2,1,0:T(8,128)S(1)} %bitcast.201, f32[1,3,2,512,512]{4,3,2,1,0:T(8,128)} %all-gather.12.cloned.1.call-done), kind=kOutput, calls=%fused_computation.33 | convolution fusion | flops 3221225472 | bytes 5242880 | tf_op jit(solution)/shard_map/dot_general | solution.py:56
  379.9 5.3 %fusion.10 = f32[512,2,512]{2,0,1:T(8,128)S(1)} fusion(f32[1,2,2,512,512]{3,4,2,1,0:T(8,128)S(1)} %bitcast.196, f32[1,3,2,512,512]{4,3,2,1,0:T(8,128)} %all-gather.12.cloned.1.call-done), kind=kOutput, calls=%fused_computation.30 | convolution fusion | flops 3221225472 | bytes 5242880 | tf_op jit(solution)/shard_map/dot_general | solution.py:53
  385.2 3.6 fusion.9
  388.8 3.6 fusion.6
  392.4 3.8 fusion.5
  396.2 3.6 subtract_bitcast_fusion
  399.8 3.6 add_bitcast_fusion
  403.4 3.8 subtract_bitcast_fusion.1
  407.3 3.6 add_bitcast_fusion.1
  410.9 3.6 subtract_bitcast_fusion.2
  414.5 3.7 add_bitcast_fusion.2
  418.2 1.6 fusion
  419.8 2.5 copy.62
  (54 shorter events, 8.1 us)
Async XLA Ops:
  6.5 201.7 %copy-start = (f32[1,8,2,64,512]{4,3,2,1,0:T(8,128)S(1)}, f32[1,8,2,64,512]{4,3,2,1,0:T(8,128)}, u32[]{:S(2)}) copy-start(f32[1,8,2,64,512]{4,3,2,1,0:T(8,128)} %param.5) | copy-start | bytes 6291460
  6.5 137.2 %all-gather.14.cloned.1.call-start = ((), (), s32[]{:S(2)}) async-start(), calls=%async_computation.1 | async-start | bytes 2359296 | tf_op jit(solution)/shard_map/all_gather | solution.py:26
  43.3 108.7 %all-gather.16.cloned.1.call-start = ((), (), s32[]{:S(2)}) async-start(), calls=%async_computation.2 | async-start | bytes 2359296 | tf_op jit(solution)/shard_map/all_gather | solution.py:26
  78.7 81.1 %all-gather.18.cloned.1.call-start = ((), (), s32[]{:S(2)}) async-start(), calls=%async_computation.3 | async-start | bytes 1966080 | tf_op jit(solution)/shard_map/all_gather | solution.py:26
  107.8 65.1 %all-gather.20.cloned.1.call-start = ((), (), s32[]{:S(2)}) async-start(), calls=%async_computation.4 | async-start | bytes 1966080 | tf_op jit(solution)/shard_map/all_gather | solution.py:26
  139.8 158.7 %all-gather.22.cloned.1.call-start = ((), (), s32[]{:S(2)}) async-start(), calls=%async_computation.5 | async-start | bytes 13369344 | tf_op jit(solution)/shard_map/all_gather | solution.py:15
  139.8 2.2 copy-start.7
  189.7 10.2 %copy-start.2 = (f32[3,1,2,512,512]{4,3,0,2,1:T(8,128)S(1)}, f32[3,1,2,512,512]{4,3,0,2,1:T(8,128)}, u32[]{:S(2)}) copy-start(f32[3,1,2,512,512]{4,3,0,2,1:T(8,128)} %broadcast_in_dim_reshape.3) | copy-start | bytes 18874372
  206.3 2.6 copy-start.8
  207.4 161.9 %all-gather.12.cloned.1.call-start = ((), (), s32[]{:S(2)}) async-start(), calls=%async_computation | async-start | bytes 7077888 | tf_op jit(solution)/shard_map/all_gather | solution.py:87
  369.2 5.7 %copy-start.5 = (f32[1,2,2,512,16,32]{3,5,4,2,1,0:T(8,128)S(1)}, f32[1,2,2,512,16,32]{3,5,4,2,1,0:T(8,128)}, u32[]{:S(2)}) copy-start(f32[1,2,2,512,16,32]{3,5,4,2,1,0:T(8,128)} %get-tuple-element.5) | copy-start | bytes 12582916
  374.9 5.0 %copy-start.4 = (f32[1,2,2,512,16,32]{3,5,4,2,1,0:T(8,128)S(1)}, f32[1,2,2,512,16,32]{3,5,4,2,1,0:T(8,128)}, u32[]{:S(2)}) copy-start(f32[1,2,2,512,16,32]{3,5,4,2,1,0:T(8,128)} %get-tuple-element.6) | copy-start | bytes 12582916
  374.9 10.3 %copy-start.6 = (f32[1,3,2,512,512]{4,3,2,1,0:T(8,128)S(1)}, f32[1,3,2,512,512]{4,3,2,1,0:T(8,128)}, u32[]{:S(2)}) copy-start(f32[1,3,2,512,512]{4,3,2,1,0:T(8,128)} %all-gather.12.cloned.1.call-done) | copy-start | bytes 18874372
  385.2 3.6 copy-start.3
  418.2 4.1 copy-start.1
Sparse Core Ops, SparseCore 0:
  43.4 21.2 all-gather.13
  78.8 36.6 all-gather.15
  117.2 27.3 all-gather.17
  146.2 26.6 all-gather.19
  207.5 91.0 all-gather.21
  300.0 69.1 all-gather.11
